TPU v7x, 32 devices: a whole 2x2x4 slice. The times are simulated.
32 devices in a mesh: clip: 16 (over z, y, x), mp: 2 (over core).
Axes of the slice: x: 2, y: 2, z: 4, core: 2. Of those that a mesh axis runs over, the one named last changes fastest.
Arguments:
- tokens: bfloat16 [48, 128, 1024], P('clip', None, 'mp'), may hold values from -6 to 6
- bottleneck: bfloat16 [16, 4, 1024], P('clip', None, 'mp'), may hold values from -6 to 6
- clip_lengths: int32 [16], replicated, may hold values from 2 to 4, as said below
- video_blocks: int32 [16], replicated, may hold values from 1 to 3, as said below
- store_map: int32 [16, 3], replicated, may hold values from -1 to 63, as said below
- norm1_gain: float32 [1024], replicated, may hold values from 0.4 to 1.6
- w_qkv: bfloat16 [3, 1024, 1024], P(None, None, 'mp'), may hold values from -0.625 to 0.625
- w_out: bfloat16 [1024, 1024], P('mp'), may hold values from -0.1875 to 0.1875
- norm2_gain: float32 [1024], replicated, may hold values from 0.4 to 1.6
- w_up: bfloat16 [1024, 4096], P(None, 'mp'), may hold values from -0.1875 to 0.1875
- w_down: bfloat16 [4096, 1024], P('mp'), may hold values from -0.09375 to 0.09375
Outputs:
- mixed_tokens: bfloat16 [48, 128, 1024], P('clip', None, 'mp')
- merged_bottleneck: bfloat16 [16, 4, 1024], P('clip', None, 'mp')
Inputs may be any that keep to these rules, and one draw needn't show every extreme that they name: clip_lengths[c] counts the blocks of the clip owned by index c of clip. The first video_blocks[c] blocks of clip c are video, the others up to clip_lengths[c] audio; video_blocks[c] <= clip_lengths[c] - 1. store_map[d, s] = c * 4 + b when slot s of device d along clip holds block b of clip c, and -1 when the slot is empty; each block b < clip_lengths[c] of each clip sits in exactly one slot, on a device of the same aligned group of 4 devices along clip as c; no device holds two blocks of one clip.
All inputs are finite; a program needn't handle non-finite values.
Results may differ from a plain program's by a relative error of at most 0.006.
Values may be sent and summed in bfloat16 or wider, within the bound.
A program may use at most 128 MiB of HBM per device.

v0:
```python
import functools

import jax
import jax.numpy as jnp
from jax import lax
from jax.experimental import pallas as pl
from jax.experimental.pallas import tpu as pltpu
from jax.sharding import PartitionSpec as P

HEAD_DIM = 64
GROUP = 4
EPS = 1e-05
NEG = -1e30
EXTRA = 16
UNROLL = True
BF16 = jnp.bfloat16
F32 = jnp.float32


def layer_norm(halves, gain):
    x = jnp.concatenate([h.astype(F32) for h in halves], axis=1)
    mean = jnp.mean(x, axis=-1, keepdims=True)
    centred = x - mean
    moment = jnp.mean(centred * centred, axis=-1, keepdims=True)
    return (centred * lax.rsqrt(moment + EPS) * gain).astype(BF16)


def dot(a, b):
    return jnp.dot(a, b, preferred_element_type=F32)


def kernel(
    blk,
    nb,
    video_ref,
    map_ref,
    tok_hbm,
    bot_ref,
    g1_ref,
    g2_ref,
    wqkv_hbm,
    wout_hbm,
    wup_hbm,
    wdown_hbm,
    out_ref,
    outb_ref,
    tok,
    wqkv,
    wout,
    wup,
    wdown,
    snd,
    x,
    ext,
    q,
    k,
    v,
    ctx,
    bias,
    ps1,
    pr1,
    own1,
    aft,
    act,
    ps2,
    pr2,
    own2,
    fin,
    ret,
    ld_sem,
    send_sem,
    recv_sem,
):
    slots = tok.shape[0]
    width = tok.shape[2]
    pairs = q.shape[0]
    keys = k.shape[1]
    rows = x.shape[1]
    ff = wup.shape[1]
    total = GROUP * blk

    me = lax.axis_index("clip")
    core = lax.axis_index("mp")
    peer = 1 - core
    bit0 = lax.rem(me, 2)
    bit1 = lax.rem(lax.div(me, 2), 2)
    flip0 = 1 - 2 * bit0
    flip1 = 2 - 4 * bit1
    partner = [me, me + flip0, me + flip1, me + flip0 + flip1]

    loads = [pltpu.make_async_copy(tok_hbm, tok, ld_sem.at[0])]
    loads.append(pltpu.make_async_copy(wqkv_hbm, wqkv, ld_sem.at[1]))
    for h in range(2):
        cols = pl.ds(h * width, width)
        loads.append(pltpu.make_async_copy(wout_hbm.at[:, cols], wout.at[h], ld_sem.at[2 + h]))
    loads.append(pltpu.make_async_copy(wup_hbm, wup, ld_sem.at[4]))
    for h in range(2):
        cols = pl.ds(h * width, width)
        loads.append(pltpu.make_async_copy(wdown_hbm.at[:, cols], wdown.at[h], ld_sem.at[5 + h]))
    loads[0].start()

    barrier = pltpu.get_barrier_semaphore()
    for r in range(1, GROUP):
        pl.semaphore_signal(barrier, inc=1, device_id={"clip": partner[r]})
    pl.semaphore_signal(barrier, inc=1, device_id={"mp": peer})

    entry = [map_ref[s, me] for s in range(slots)]
    own = [jnp.where(e >= 0, lax.div(e, GROUP), -1) for e in entry]
    pick = []
    for r in range(GROUP):
        chosen = jnp.int32(0)
        for s in range(slots):
            chosen = jnp.where(own[s] == partner[r], s, chosen)
        pick.append(chosen)
    video = video_ref[me]
    mode = []
    for r in range(GROUP):
        m = jnp.int32(-1)
        for s in range(slots):
            e = map_ref[s, partner[r]]
            mine = (e >= 0) & (lax.div(e, GROUP) == me)
            m = jnp.where(mine, jnp.where(lax.rem(e, GROUP) < video, 0, 1), m)
        mode.append(m)

    place = [(GROUP - 1) * blk] + [(r - 1) * blk for r in range(1, GROUP)]
    span = [pl.ds(place[0], blk + EXTRA)] + [pl.ds(place[r], blk) for r in range(1, GROUP)]
    size = [blk + EXTRA] + [blk] * (GROUP - 1)

    def ici(r, src, dst, base):
        return pltpu.make_async_remote_copy(
            src_ref=src,
            dst_ref=dst,
            send_sem=send_sem.at[base + r],
            recv_sem=recv_sem.at[base + r],
            device_id={"clip": partner[r]},
        )

    def d2d(r, src, dst, base):
        return pltpu.make_async_remote_copy(
            src_ref=src,
            dst_ref=dst,
            send_sem=send_sem.at[base + r],
            recv_sem=recv_sem.at[base + r],
            device_id={"mp": peer},
        )

    half = x.at[core]
    arrive = [ici(r, snd.at[r - 1], half.at[span[r]], 0) if r else None for r in range(GROUP)]
    share = [d2d(r, half.at[span[r]], half.at[span[r]], 4) for r in range(GROUP)]
    proj = [d2d(r, ps1.at[span[r]], pr1.at[span[r]], 8) for r in range(GROUP)]
    joined = [d2d(r, aft.at[core].at[span[r]], aft.at[core].at[span[r]], 12) for r in range(GROUP)]
    down = [d2d(r, ps2.at[span[r]], pr2.at[span[r]], 16) for r in range(GROUP)]
    back = [ici(r, fin.at[r - 1], ret.at[r], 20) if r else None for r in range(GROUP)]

    loads[0].wait()
    for r in range(1, GROUP):
        snd[r - 1] = tok[pick[r]]
    x[core, pl.ds(place[0], blk)] = tok[pick[0]]
    small = bot_ref[0].astype(F32)
    for i in range(EXTRA // nb):
        ext[pl.ds(i * nb, nb)] = small
    x[core, pl.ds(total, EXTRA)] = ext[...].astype(BF16)

    pl.semaphore_wait(barrier, GROUP)
    for r in (1, 2, 3):
        arrive[r].start()
    share[0].start()
    for load in loads[1:]:
        load.start()

    column = lax.broadcasted_iota(jnp.int32, (1, keys), 1)
    extra_key = (column >= total) & (column < total + nb)
    key_mode = jnp.full((1, keys), -1, jnp.int32)
    for r in range(GROUP):
        inside = (column >= place[r]) & (column < place[r] + blk)
        key_mode = jnp.where(inside, mode[r], key_mode)

    def bias_of(m):
        return jnp.where(extra_key | ((key_mode == m) & (key_mode >= 0)), 0.0, NEG).astype(F32)

    row_bias = [bias_of(mode[r]) for r in range(GROUP)]
    bias[pl.ds(0, blk)] = jnp.broadcast_to(row_bias[0], (blk, keys))
    line = lax.broadcasted_iota(jnp.int32, (EXTRA, keys), 0)
    bias[pl.ds(blk, EXTRA)] = jnp.where(
        (line >= nb) & (line < 2 * nb),
        jnp.broadcast_to(bias_of(1), (EXTRA, keys)),
        jnp.broadcast_to(bias_of(0), (EXTRA, keys)),
    )
    for j in range(pairs):
        k[j, pl.ds(rows, keys - rows)] = jnp.zeros((keys - rows, 128), BF16)
        v[j, pl.ds(rows, keys - rows), :128] = jnp.zeros((keys - rows, 128), BF16)
        v[j, :, 128:] = jnp.ones((keys, 128), BF16)

    def project(r):
        n = layer_norm([x[0, span[r]], x[1, span[r]]], g1_ref[...])
        for i, target in enumerate((q, k, v)):
            y = dot(n, wqkv[i])
            if i == 0:
                y = y.astype(BF16).astype(F32) * HEAD_DIM ** (-0.5)
            y = y.astype(BF16)
            for j in range(pairs):
                target[j, span[r], :128] = y[:, j * 128 : (j + 1) * 128]

    loads[1].wait()
    share[0].wait_recv()
    project(0)
    for r in (1, 2):
        arrive[r].wait_recv()
        share[r].start()
    for r in (1, 2):
        share[r].wait_recv()
        project(r)
    arrive[3].wait_recv()
    share[3].start()
    share[3].wait_recv()
    project(3)

    def attend(r):
        lane = lax.broadcasted_iota(jnp.int32, (1, 128), 1)
        low = lane < HEAD_DIM

        def step(j, _):
            qs = q[j, span[r]]
            zero = jnp.zeros_like(qs)
            both = jnp.concatenate([jnp.where(low, qs, zero), jnp.where(low, zero, qs)], axis=0)
            s = lax.dot_general(both, k[j], (((1,), (1,)), ((), ())), preferred_element_type=F32)
            if r == 0:
                b = bias[...]
                s = s + jnp.concatenate([b, b], axis=0)
            else:
                s = s + row_bias[r]
            top = jnp.max(s, axis=-1, keepdims=True)
            p = jnp.exp(s - top).astype(BF16)
            o = dot(p, v[j])
            m = size[r]
            over = jnp.where(low, o[:m, :128], o[m:, :128])
            under = jnp.where(low, o[:m, 128:], o[m:, 128:])
            o = over / under
            if r == 0:
                ctx[j, pl.ds(place[0], blk)] = o[:blk].astype(BF16)
                e = o[blk:]
                e = 0.5 * (e + pltpu.roll(e, EXTRA - nb, 0))
                ctx[j, pl.ds(total, EXTRA)] = e.astype(BF16)
            else:
                ctx[j, span[r]] = o.astype(BF16)
            return 0

        lax.fori_loop(0, pairs, step, 0, unroll=UNROLL)

    def stage_a(r):
        attend(r)
        c = jnp.concatenate([ctx[j, span[r]] for j in range(pairs)], axis=1)
        ps1[span[r]] = dot(c, wout[peer]).astype(BF16)
        proj[r].start()
        own1[span[r]] = dot(c, wout[core])

    def stage_b(r):
        proj[r].wait_recv()
        total_sum = x[core, span[r]].astype(F32) + (own1[span[r]] + pr1[span[r]].astype(F32))
        aft[core, span[r]] = total_sum.astype(BF16)
        joined[r].start()

    def stage_c(r):
        joined[r].wait_recv()
        n = layer_norm([aft[0, span[r]], aft[1, span[r]]], g2_ref[...])
        tile = width
        for t in range(ff // tile):
            up = dot(n, wup[:, t * tile : (t + 1) * tile])
            act[pl.ds(0, size[r]), t * tile : (t + 1) * tile] = jax.nn.gelu(up, approximate=True).astype(BF16)
        a = act[pl.ds(0, size[r])]
        ps2[span[r]] = dot(a, wdown[peer]).astype(BF16)
        down[r].start()
        own2[span[r]] = dot(a, wdown[core])

    def stage_d(r):
        down[r].wait_recv()
        merged = aft[core, span[r]].astype(F32) + (own2[span[r]] + pr2[span[r]].astype(F32))
        if r == 0:
            ret[0] = merged[:blk].astype(BF16)
            outb_ref[0] = merged[blk : blk + nb].astype(BF16)
        else:
            fin[r - 1] = merged.astype(BF16)
            back[r].start()

    loads[2].wait()
    loads[3].wait()
    stage_a(3)
    stage_a(1)
    stage_b(3)
    stage_a(2)
    stage_b(1)
    for load in loads[4:]:
        load.wait()
    stage_c(3)
    stage_a(0)
    stage_b(2)
    stage_d(3)
    stage_c(1)
    stage_b(0)
    stage_d(1)
    stage_c(2)
    stage_d(2)
    stage_c(0)
    stage_d(0)
    for r in (3, 1, 2):
        back[r].wait_recv()
    for s in range(slots):
        where = jnp.int32(0)
        for r in range(GROUP):
            where = jnp.where(own[s] == partner[r], r, where)
        live = jnp.where(entry[s] >= 0, 1.0, 0.0).astype(F32)
        block = ret[where].astype(F32)
        out_ref[s] = (block * live).astype(BF16)
    for r in range(1, GROUP):
        arrive[r].wait_send()
        back[r].wait_send()
    for r in range(GROUP):
        for c in (share, proj, joined, down):
            c[r].wait_send()


def place(stored_ref, merged_ref, out_ref, outb_ref):
    out_ref[...] = stored_ref[...]
    outb_ref[...] = merged_ref[...]


def body(
    tokens,
    bottleneck,
    clip_lengths,
    video_blocks,
    store_map,
    norm1_gain,
    w_qkv,
    w_out,
    norm2_gain,
    w_up,
    w_down,
):
    slots, blk, width = tokens.shape
    nb = bottleneck.shape[1]
    dim = w_qkv.shape[1]
    inner = w_qkv.shape[2]
    ff = w_up.shape[1]
    pairs = inner // 128
    rows = GROUP * blk + EXTRA
    keys = (rows + 127) // 128 * 128
    smem = pl.BlockSpec(memory_space=pltpu.SMEM)
    vmem = pl.BlockSpec(memory_space=pltpu.VMEM)
    hbm = pl.BlockSpec(memory_space=pl.ANY)
    V = pltpu.VMEM
    stored, merged = pl.pallas_call(
        functools.partial(kernel, blk, nb),
        out_shape=(
            jax.ShapeDtypeStruct(tokens.shape, BF16),
            jax.ShapeDtypeStruct(bottleneck.shape, BF16),
        ),
        in_specs=[smem, smem, hbm, vmem, vmem, vmem, hbm, hbm, hbm, hbm],
        out_specs=(vmem, vmem),
        scratch_shapes=[
            V((slots, blk, width), BF16),
            V(w_qkv.shape, BF16),
            V((2, inner, width), BF16),
            V(w_up.shape, BF16),
            V((2, ff, width), BF16),
            V((GROUP - 1, blk, width), BF16),
            V((2, rows, width), BF16),
            V((EXTRA, width), F32),
            V((pairs, rows, 128), BF16),
            V((pairs, keys, 128), BF16),
            V((pairs, keys, 256), BF16),
            V((pairs, rows, 128), BF16),
            V((blk + EXTRA, keys), F32),
            V((rows, width), BF16),
            V((rows, width), BF16),
            V((rows, width), F32),
            V((2, rows, width), BF16),
            V((blk + EXTRA, ff), BF16),
            V((rows, width), BF16),
            V((rows, width), BF16),
            V((rows, width), F32),
            V((GROUP - 1, blk, width), BF16),
            V((GROUP, blk, width), BF16),
            pltpu.SemaphoreType.DMA((7,)),
            pltpu.SemaphoreType.DMA((24,)),
            pltpu.SemaphoreType.DMA((24,)),
        ],
        compiler_params=pltpu.CompilerParams(collective_id=0, has_side_effects=True),
        name="merge_layer",
    )(
        video_blocks,
        store_map.T,
        tokens,
        bottleneck,
        norm1_gain.reshape(1, dim),
        norm2_gain.reshape(1, dim),
        w_qkv,
        w_out,
        w_up,
        w_down,
    )
    return pl.pallas_call(
        place,
        out_shape=(
            jax.ShapeDtypeStruct(tokens.shape, BF16),
            jax.ShapeDtypeStruct(bottleneck.shape, BF16),
        ),
        in_specs=[vmem, vmem],
        out_specs=(vmem, vmem),
        name="place",
    )(stored, merged)


def solution(mesh):
    placed = (
        P("clip", None, "mp"),
        P("clip", None, "mp"),
        P(),
        P(),
        P(),
        P(),
        P(None, None, "mp"),
        P("mp", None),
        P(),
        P(None, "mp"),
        P("mp", None),
    )
    return jax.shard_map(
        body,
        mesh=mesh,
        in_specs=placed,
        out_specs=(P("clip", None, "mp"), P("clip", None, "mp")),
        check_vma=False,
    )
```

profile of v0, /device:TPU:0, one launch (start us, length us, event | category | flops | bytes accessed | tf_op | source)
XLA Modules:
  0.0 36.8 jit_solution(16674849684625015356)
XLA Ops:
  0.6 34.4 %merge_layer.1 = (bf16[3,128,512]{2,1,0:T(8,128)(2,1)}, bf16[1,4,512]{2,1,0:T(4,128)(2,1)}) custom-call(s32[16]{0:T(128)} %video_ref.1, s32[3,16]{1,0:T(4,128)} %bitcast.5, bf16[3,128,512]{2,1,0:T(8,128)(2,1)} %tok_hbm.1, bf16[1,4,512]{2,1,0:T(4,128)(2,1)} %bot_ref.1, f32[1,1024]{1,0:T(1,128)} %bitcast.3, f32[1,1024]{1,0:T(1,128)} %bitcast.4, ...), custom_call_target="tpu_custom_call" | custom-call | tf_op jit(solution)/shard_map/merge_layer/pallas_call | solution.py:352
  35.1 1.8 %place.1 = (bf16[3,128,512]{2,1,0:T(8,128)(2,1)}, bf16[1,4,512]{2,1,0:T(4,128)(2,1)}) custom-call(bf16[3,128,512]{2,1,0:T(8,128)(2,1)} %get-tuple-element.4.stored_ref, bf16[1,4,512]{2,1,0:T(4,128)(2,1)} %get-tuple-element.5.merged_ref), custom_call_target="tpu_custom_call" | custom-call | tf_op jit(solution)/shard_map/place/pallas_call | solution.py:402
where the time goes:
time: 37.1 us; the launch traced here: 36.8 us
  Pallas kernels  36.2 us (98%)
  between operations  0.64 us (2%)
    pallas_call x1, Pallas kernels, body(): pl.pallas_call(functools.partial(kernel, blk, nb), out_shape=(jax.ShapeDt...  34.4 us
    pallas_call x1, Pallas kernels, body(): pl.pallas_call(place, out_shape=(jax.ShapeDtypeStruct(tokens.shape, BF16)...  1.77 us

commit v1 on v0

v1 whole, which is shorter than its diff:
```python
import functools

import jax
import jax.numpy as jnp
from jax import lax
from jax.experimental import pallas as pl
from jax.experimental.pallas import tpu as pltpu
from jax.sharding import PartitionSpec as P

HEAD_DIM = 64
GROUP = 4
EPS = 1e-05
NEG = -1e30
EXTRA = 16
LOG2E = 1.4426950408889634
GELU = 0.7978845608028654
LOOK = 2
SCOPE = jax.named_scope
BF16 = jnp.bfloat16
F32 = jnp.float32


def layer_norm(halves, gain):
    x = jnp.concatenate([h.astype(F32) for h in halves], axis=1)
    mean = jnp.mean(x, axis=-1, keepdims=True)
    centred = x - mean
    moment = jnp.mean(centred * centred, axis=-1, keepdims=True)
    return (centred * lax.rsqrt(moment + EPS) * gain).astype(BF16)


def dot(a, b):
    return jnp.dot(a, b, preferred_element_type=F32)


def gelu(y):
    rate = y * (0.044715 * GELU * (y * y) + GELU)
    half = 0.5 * y
    return half + half * jnp.tanh(rate)


def kernel(
    blk,
    nb,
    video_hbm,
    map_hbm,
    tok_hbm,
    bot_hbm,
    g1_hbm,
    g2_hbm,
    wqkv_hbm,
    wout_hbm,
    wup_hbm,
    wdown_hbm,
    out_ref,
    outb_ref,
    video_ref,
    map_ref,
    bot_ref,
    g1_ref,
    g2_ref,
    tok,
    wqkv,
    wout,
    wup,
    wdown,
    snd,
    x,
    ext,
    qm,
    qb,
    k,
    vt,
    ctx,
    ps1,
    pr1,
    own1,
    aft,
    act,
    ps2,
    pr2,
    own2,
    fin,
    ret,
    ld_sem,
    send_sem,
    recv_sem,
):
    slots = tok.shape[0]
    width = tok.shape[2]
    pairs = vt.shape[0]
    keys = vt.shape[2]
    rows = x.shape[1]
    ff = wdown.shape[1]
    total = GROUP * blk

    me = lax.axis_index("clip")
    core = lax.axis_index("mp")
    peer = 1 - core
    bit0 = lax.rem(me, 2)
    bit1 = lax.rem(lax.div(me, 2), 2)
    flip0 = 1 - 2 * bit0
    flip1 = 2 - 4 * bit1
    partner = [me, me + flip0, me + flip1, me + flip0 + flip1]

    barrier = pltpu.get_barrier_semaphore()
    for r in range(1, GROUP):
        pl.semaphore_signal(barrier, inc=1, device_id={"clip": partner[r]})
    pl.semaphore_signal(barrier, inc=1, device_id={"mp": peer})

    def load(i, src, dst):
        return pltpu.make_async_copy(src, dst, ld_sem.at[i])

    halves = [pl.ds(h * width, width) for h in range(2)]
    first = [
        load(0, tok_hbm, tok),
        load(1, map_hbm, map_ref),
        load(2, video_hbm, video_ref),
        load(3, bot_hbm, bot_ref),
        load(4, g1_hbm, g1_ref),
        load(5, g2_hbm, g2_ref),
    ]
    load_qkv = load(6, wqkv_hbm, wqkv)
    tiles = wup.shape[0]
    load_out = [load(7 + h, wout_hbm.at[:, halves[h]], wout.at[h]) for h in range(2)]
    load_down = [load(9 + h, wdown_hbm.at[:, halves[h]], wdown.at[h]) for h in range(2)]
    load_up = [load(11 + t, wup_hbm.at[:, pl.ds(t * width, width)], wup.at[t]) for t in range(tiles)]
    for c in first:
        c.start()

    column = lax.broadcasted_iota(jnp.int32, (1, width), 1)
    low = lax.rem(column, 2 * HEAD_DIM) < HEAD_DIM
    for j in range(pairs):
        vt[j, 2 * HEAD_DIM :] = jnp.ones((EXTRA, keys), BF16)

    for c in first:
        c.wait()
    for c in (load_qkv, *load_out, *load_up, *load_down):
        c.start()

    entry = [map_ref[s, me] for s in range(slots)]
    own = [jnp.where(e >= 0, lax.div(e, GROUP), -1) for e in entry]
    pick = []
    for r in range(GROUP):
        chosen = jnp.int32(0)
        for s in range(slots):
            chosen = jnp.where(own[s] == partner[r], s, chosen)
        pick.append(chosen)
    video = video_ref[me]
    mode = []
    for r in range(GROUP):
        m = jnp.int32(-1)
        for s in range(slots):
            e = map_ref[s, partner[r]]
            mine = (e >= 0) & (lax.div(e, GROUP) == me)
            m = jnp.where(mine, jnp.where(lax.rem(e, GROUP) < video, 0, 1), m)
        mode.append(m)

    order = [1, 2, 3, 0]
    place = [(GROUP - 1) * blk] + [(r - 1) * blk for r in range(1, GROUP)]
    span = [pl.ds(place[0], blk + EXTRA)] + [pl.ds(place[r], blk) for r in range(1, GROUP)]

    def ici(r, src, dst, base):
        return pltpu.make_async_remote_copy(
            src_ref=src,
            dst_ref=dst,
            send_sem=send_sem.at[base + r],
            recv_sem=recv_sem.at[base + r],
            device_id={"clip": partner[r]},
        )

    def d2d(r, src, dst, base):
        return pltpu.make_async_remote_copy(
            src_ref=src,
            dst_ref=dst,
            send_sem=send_sem.at[base + r],
            recv_sem=recv_sem.at[base + r],
            device_id={"mp": peer},
        )

    half = x.at[core]
    arrive = [ici(r, snd.at[r - 1], half.at[span[r]], 0) if r else None for r in range(GROUP)]
    share = [d2d(r, half.at[span[r]], half.at[span[r]], 4) for r in range(GROUP)]
    proj = [d2d(r, ps1.at[:, span[r]], pr1.at[:, span[r]], 8) for r in range(GROUP)]
    down = [d2d(r, ps2.at[span[r]], pr2.at[span[r]], 12) for r in range(GROUP)]
    back = [ici(r, fin.at[r - 1], ret.at[r], 16) if r else None for r in range(GROUP)]

    for r in range(1, GROUP):
        snd[r - 1] = tok[pick[r]]
    x[core, pl.ds(place[0], blk)] = tok[pick[0]]
    small = bot_ref[0].astype(F32)
    for i in range(EXTRA // nb):
        ext[pl.ds(i * nb, nb)] = small
    x[core, pl.ds(total, EXTRA)] = ext[...].astype(BF16)

    with SCOPE("barrier"):
        pl.semaphore_wait(barrier, GROUP)
    for r in (1, 2, 3):
        arrive[r].start()
    share[0].start()

    def seen(m, s):
        return jnp.where((mode[s] == m) & (mode[s] >= 0), 0.0, NEG).astype(F32)

    tail = lax.broadcasted_iota(jnp.int32, (EXTRA, 1), 0) < nb

    def project(r):
        n = layer_norm([x[0, span[r]], x[1, span[r]]], g1_ref[...])
        y = dot(n, wqkv[0]) * (HEAD_DIM ** (-0.5) * LOG2E)
        y0 = jnp.where(low, y, 0.0).astype(BF16)
        y1 = jnp.where(low, 0.0, y).astype(BF16)
        qm[0, span[r]] = y0
        qm[1, span[r]] = y1
        if r == 0:
            e = y[blk:]
            head = lax.div(column, HEAD_DIM)
            for h in range(2 * pairs):
                qb[pl.ds(h * EXTRA, EXTRA)] = jnp.where(head == h, e, 0.0).astype(BF16)
        k[span[r]] = dot(n, wqkv[1]).astype(BF16)
        y = dot(n, wqkv[2])
        for j in range(pairs):
            cols = y[:, j * 128 : (j + 1) * 128]
            vt[j, :128, pl.ds(place[r], blk)] = cols[:blk].T.astype(BF16)
            if r == 0:
                padded = jnp.concatenate([cols[blk:], jnp.zeros((128 - EXTRA, 128), F32)], axis=0)
                vt[j, :128, pl.ds(total, 128)] = padded.T.astype(BF16)

    def soften(s, bias):
        n = s.shape[1]
        parts = [s[p * blk : (p + 1) * blk] for p in range(GROUP)]
        last = jnp.where(tail, s[total:], NEG)
        tops = [jnp.max(p.reshape(blk // 8, 8, n), axis=0) + b for p, b in zip(parts, bias)]
        tops.append(jnp.max(last.reshape(EXTRA // 8, 8, n), axis=0))
        top = tops[0]
        for t in tops[1:]:
            top = jnp.maximum(top, t)
        top = jnp.max(top, axis=0, keepdims=True)
        p = [jnp.exp2(q + (b - top)).astype(BF16) for q, b in zip(parts, bias)]
        p.append(jnp.exp2(last - top).astype(BF16))
        p.append(jnp.zeros((keys - rows, n), BF16))
        return jnp.concatenate(p, axis=0)

    def scores(a, b):
        return lax.dot_general(a, b, (((1,), (1,)), ((), ())), preferred_element_type=F32)

    def score(item):
        r, j = item
        if r is None:
            return scores(k[...], qb[...])
        at = pl.ds(place[r], blk)
        cols = slice(j * 128, (j + 1) * 128)
        both = jnp.concatenate([qm[0, at, cols], qm[1, at, cols]], axis=0)
        return scores(k[:, cols], both)

    def mix(item, s):
        r, j = item
        if r is None:
            mix_small(s)
            return
        at = pl.ds(place[r], blk)
        cols = slice(j * 128, (j + 1) * 128)
        p = soften(s, [seen(mode[r], b) for b in order])
        o = dot(vt[j], p)
        under = 1.0 / o[128:129]
        d = HEAD_DIM
        o = jnp.concatenate([o[:d, :blk] * under[:, :blk], o[d : 2 * d, blk:] * under[:, blk:]], axis=0)
        ctx[at, cols] = o.T.astype(BF16)

    def mix_small(s):
        n = 2 * pairs * EXTRA
        step = lax.rem(lax.broadcasted_iota(jnp.int32, (1, n), 1), EXTRA)
        audio = (step >= nb) & (step < 2 * nb)
        p = soften(s, [jnp.where(audio, seen(1, b), seen(0, b)) for b in order])
        for j in range(pairs):
            o = dot(vt[j], p)
            o = (o[:128] * (1.0 / o[128:129])).T
            at = 2 * j * EXTRA
            e = jnp.where(low[:, :128], o[at : at + EXTRA], o[at + EXTRA : at + 2 * EXTRA])
            e = 0.5 * (e + pltpu.roll(e, EXTRA - nb, 0))
            ctx[pl.ds(total, EXTRA), j * 128 : (j + 1) * 128] = e.astype(BF16)

    def project_out(r):
        c = ctx[span[r]]
        for h in range(2):
            y = dot(c, wout[h])
            ps1[h, span[r]] = y.astype(BF16)
            own1[h, span[r]] = y
        proj[r].start()

    def normed_after(r):
        at = span[r]
        parts = []
        for h in range(2):
            t = x[h, at].astype(F32) + (own1[h, at] + pr1[h, at].astype(F32))
            t = t.astype(BF16)
            aft[h, at] = t
            parts.append(t)
        return layer_norm(parts, g2_ref[...])

    def grow(r, n):
        for t in range(tiles):
            act[span[r], t * width : (t + 1) * width] = gelu(dot(n, wup[t])).astype(BF16)

    def shrink(r):
        a = act[span[r]]
        ps2[span[r]] = dot(a, wdown[peer]).astype(BF16)
        down[r].start()
        own2[span[r]] = dot(a, wdown[core])

    def finish(r):
        at = span[r]
        merged = aft[core, at].astype(F32) + (own2[at] + pr2[at].astype(F32))
        if r == 0:
            ret[0] = merged[:blk].astype(BF16)
            outb_ref[0] = merged[blk : blk + nb].astype(BF16)
        else:
            fin[r - 1] = merged.astype(BF16)
            back[r].start()

    with SCOPE("w0"):
        load_qkv.wait()
        share[0].wait_recv()
    with SCOPE("project0"):
        project(0)
    for r in (1, 2):
        with SCOPE("arr%d" % r):
            arrive[r].wait_recv()
        share[r].start()
    for r in (1, 2):
        with SCOPE("sh%d" % r):
            share[r].wait_recv()
        with SCOPE("project%d" % r):
            project(r)
    with SCOPE("arr3"):
        arrive[3].wait_recv()
    share[3].start()
    with SCOPE("ldwait"):
        for c in (*load_out, *load_up, *load_down):
            c.wait()
    with SCOPE("sh3"):
        share[3].wait_recv()
    items = [(r, j) for r in (3, 1, 2, 0) for j in range(pairs)]
    items.insert(3 * pairs, (None, 0))
    emit_out = {(1, 1): 3, (2, 1): 1, (0, 1): 2}
    with SCOPE("attention"):
        project(3)
        waiting = {}
        for t in range(len(items) + LOOK):
            if t < len(items):
                waiting[t] = score(items[t])
            if t >= LOOK:
                mix(items[t - LOOK], waiting.pop(t - LOOK))
                if items[t - LOOK] in emit_out:
                    project_out(emit_out[items[t - LOOK]])
        project_out(0)
    with SCOPE("wproj31"):
        proj[3].wait_recv()
        proj[1].wait_recv()
    with SCOPE("ffnA"):
        grow(3, normed_after(3))
        n = normed_after(1)
        shrink(3)
        grow(1, n)
    with SCOPE("wB"):
        proj[2].wait_recv()
        down[3].wait_recv()
    with SCOPE("ffnB"):
        finish(3)
        n = normed_after(2)
        shrink(1)
        grow(2, n)
    with SCOPE("wC"):
        proj[0].wait_recv()
        down[1].wait_recv()
    with SCOPE("ffnC"):
        finish(1)
        n = normed_after(0)
        shrink(2)
        grow(0, n)
    with SCOPE("wD"):
        down[2].wait_recv()
    with SCOPE("ffnD"):
        finish(2)
        shrink(0)
    with SCOPE("wE"):
        down[0].wait_recv()
    with SCOPE("fin0"):
        finish(0)
    with SCOPE("backwait"):
        for r in (3, 1, 2):
            back[r].wait_recv()
    for s in range(slots):
        where = jnp.int32(0)
        for r in range(GROUP):
            where = jnp.where(own[s] == partner[r], r, where)
        live = jnp.where(entry[s] >= 0, 1.0, 0.0).astype(F32)
        block = ret[where].astype(F32)
        out_ref[s] = (block * live).astype(BF16)
    for r in range(1, GROUP):
        arrive[r].wait_send()
        back[r].wait_send()
    for r in range(GROUP):
        for c in (share, proj, down):
            c[r].wait_send()


def place(stored_ref, merged_ref, out_ref, outb_ref):
    out_ref[...] = stored_ref[...]
    outb_ref[...] = merged_ref[...]


def body(
    tokens,
    bottleneck,
    clip_lengths,
    video_blocks,
    store_map,
    norm1_gain,
    w_qkv,
    w_out,
    norm2_gain,
    w_up,
    w_down,
):
    slots, blk, width = tokens.shape
    nb = bottleneck.shape[1]
    dim = w_qkv.shape[1]
    inner = w_qkv.shape[2]
    ff = w_up.shape[1]
    pairs = inner // 128
    rows = GROUP * blk + EXTRA
    keys = (rows + 127) // 128 * 128
    vmem = pl.BlockSpec(memory_space=pltpu.VMEM)
    hbm = pl.BlockSpec(memory_space=pltpu.HBM)
    V = pltpu.VMEM
    stored, merged = pl.pallas_call(
        functools.partial(kernel, blk, nb),
        out_shape=(
            jax.ShapeDtypeStruct(tokens.shape, BF16),
            jax.ShapeDtypeStruct(bottleneck.shape, BF16),
        ),
        in_specs=[hbm] * 10,
        out_specs=(vmem, vmem),
        scratch_shapes=[
            pltpu.SMEM(video_blocks.shape, jnp.int32),
            pltpu.SMEM(store_map.shape[::-1], jnp.int32),
            V(bottleneck.shape, BF16),
            V((1, dim), F32),
            V((1, dim), F32),
            V((slots, blk, width), BF16),
            V(w_qkv.shape, BF16),
            V((2, inner, width), BF16),
            V((ff // width, dim, width), BF16),
            V((2, ff, width), BF16),
            V((GROUP - 1, blk, width), BF16),
            V((2, rows, width), BF16),
            V((EXTRA, width), F32),
            V((2, rows, inner), BF16),
            V((2 * pairs * EXTRA, inner), BF16),
            V((rows, inner), BF16),
            V((pairs, 128 + EXTRA, keys), BF16),
            V((rows, inner), BF16),
            V((2, rows, width), BF16),
            V((2, rows, width), BF16),
            V((2, rows, width), F32),
            V((2, rows, width), BF16),
            V((rows, ff), BF16),
            V((rows, width), BF16),
            V((rows, width), BF16),
            V((rows, width), F32),
            V((GROUP - 1, blk, width), BF16),
            V((GROUP, blk, width), BF16),
            pltpu.SemaphoreType.DMA((11 + ff // width,)),
            pltpu.SemaphoreType.DMA((20,)),
            pltpu.SemaphoreType.DMA((20,)),
        ],
        compiler_params=pltpu.CompilerParams(collective_id=0, has_side_effects=True, vmem_limit_bytes=40 << 20),
        name="merge_layer",
    )(
        *(
            pltpu.with_memory_space_constraint(a, pltpu.HBM)
            for a in (
                video_blocks,
                store_map.T,
                tokens,
                bottleneck,
                norm1_gain.reshape(1, dim),
                norm2_gain.reshape(1, dim),
                w_qkv,
                w_out,
                w_up,
                w_down,
            )
        )
    )
    return pl.pallas_call(
        place,
        out_shape=(
            jax.ShapeDtypeStruct(tokens.shape, BF16),
            jax.ShapeDtypeStruct(bottleneck.shape, BF16),
        ),
        in_specs=[vmem, vmem],
        out_specs=(vmem, vmem),
        compiler_params=pltpu.CompilerParams(vmem_limit_bytes=4 << 20),
        name="place",
    )(stored, merged)


def solution(mesh):
    placed = (
        P("clip", None, "mp"),
        P("clip", None, "mp"),
        P(),
        P(),
        P(),
        P(),
        P(None, None, "mp"),
        P("mp", None),
        P(),
        P(None, "mp"),
        P("mp", None),
    )
    return jax.shard_map(
        body,
        mesh=mesh,
        in_specs=placed,
        out_specs=(P("clip", None, "mp"), P("clip", None, "mp")),
        check_vma=False,
    )
```

time: 37.1 us -> 31 us (0.84)
  Pallas kernels: 36.2 us -> 30.2 us
    pallas_call x1, Pallas kernels: 34.4 us -> 29.5 us  [body(): pl.pallas_call(functools.partial(kernel, blk, nb), out_shape=(jax.ShapeDt...]
    pallas_call x1, Pallas kernels: 1.77 us -> 0.77 us  [body(): pl.pallas_call(place, out_shape=(jax.ShapeDtypeStruct(tokens.shape, BF16)...]
where the time goes in v1:
time: 31 us; the launch traced here: 30.9 us
  Pallas kernels  30.2 us (97%)
  between operations  0.64 us (2%)
    pallas_call x1, Pallas kernels, body(): pl.pallas_call(functools.partial(kernel, blk, nb), out_shape=(jax.ShapeDt...  29.5 us
    pallas_call x1, Pallas kernels, body(): pl.pallas_call(place, out_shape=(jax.ShapeDtypeStruct(tokens.shape, BF16)...  0.77 us

profile of v1, /device:TPU:0, one launch (start us, length us, event | category | flops | bytes accessed | tf_op | source)
XLA Modules:
  0.0 30.9 jit_solution(11697124484808283597)
XLA Ops:
  0.6 29.5 %merge_layer.1 = (bf16[3,128,512]{2,1,0:T(8,128)(2,1)S(1)}, bf16[1,4,512]{2,1,0:T(4,128)(2,1)S(1)}) custom-call(s32[16]{0:T(128)} %video_hbm.1, s32[3,16]{1,0:T(4,128)} %bitcast.5, bf16[3,128,512]{2,1,0:T(8,128)(2,1)} %tok_hbm.1, bf16[1,4,512]{2,1,0:T(4,128)(2,1)} %bot_hbm.1, f32[1,1024]{1,0:T(1,128)} %bitcast.3, f32[1,1024]{1,0:T(1,128)} %bitcast.4, ...), custom_call_target="tpu_custom_call" | custom-call | tf_op jit(solution)/shard_map/merge_layer/pallas_call | solution.py:435
  30.1 0.8 %place.1 = (bf16[3,128,512]{2,1,0:T(8,128)(2,1)}, bf16[1,4,512]{2,1,0:T(4,128)(2,1)}) custom-call(bf16[3,128,512]{2,1,0:T(8,128)(2,1)S(1)} %get-tuple-element.4.stored_ref, bf16[1,4,512]{2,1,0:T(4,128)(2,1)S(1)} %get-tuple-element.5.merged_ref), custom_call_target="tpu_custom_call" | custom-call | tf_op jit(solution)/shard_map/place/pallas_call | solution.py:495

commit v2 on v1

--- a/solution.py
+++ b/solution.py
@@ -70,6 +70,8 @@
     qb,
     k,
     vt,
+    part,
+    part_top,
     ctx,
     ps1,
     pr1,
@@ -91,7 +93,6 @@
     keys = vt.shape[2]
     rows = x.shape[1]
     ff = wdown.shape[1]
-    total = GROUP * blk
 
     me = lax.axis_index("clip")
     core = lax.axis_index("mp")
@@ -155,8 +156,11 @@
             m = jnp.where(mine, jnp.where(lax.rem(e, GROUP) < video, 0, 1), m)
         mode.append(m)
 
-    order = [1, 2, 3, 0]
-    place = [(GROUP - 1) * blk] + [(r - 1) * blk for r in range(1, GROUP)]
+    order = [1, 2, 0]
+    total = (GROUP - 1) * blk
+    late = total + EXTRA
+    place = [2 * blk, 0, blk, late]
+    lanes = [2 * blk, 0, blk, total + 128]
     span = [pl.ds(place[0], blk + EXTRA)] + [pl.ds(place[r], blk) for r in range(1, GROUP)]
 
     def ici(r, src, dst, base):
@@ -203,8 +207,10 @@
 
     tail = lax.broadcasted_iota(jnp.int32, (EXTRA, 1), 0) < nb
 
-    def project(r):
-        n = layer_norm([x[0, span[r]], x[1, span[r]]], g1_ref[...])
+    def norm(r):
+        return layer_norm([x[0, span[r]], x[1, span[r]]], g1_ref[...])
+
+    def project(r, n, then=None):
         y = dot(n, wqkv[0]) * (HEAD_DIM ** (-0.5) * LOG2E)
         y0 = jnp.where(low, y, 0.0).astype(BF16)
         y1 = jnp.where(low, 0.0, y).astype(BF16)
@@ -216,67 +222,108 @@
             for h in range(2 * pairs):
                 qb[pl.ds(h * EXTRA, EXTRA)] = jnp.where(head == h, e, 0.0).astype(BF16)
         k[span[r]] = dot(n, wqkv[1]).astype(BF16)
+        if then is not None:
+            then()
         y = dot(n, wqkv[2])
         for j in range(pairs):
             cols = y[:, j * 128 : (j + 1) * 128]
-            vt[j, :128, pl.ds(place[r], blk)] = cols[:blk].T.astype(BF16)
+            vt[j, :128, pl.ds(lanes[r], blk)] = cols[:blk].T.astype(BF16)
             if r == 0:
                 padded = jnp.concatenate([cols[blk:], jnp.zeros((128 - EXTRA, 128), F32)], axis=0)
                 vt[j, :128, pl.ds(total, 128)] = padded.T.astype(BF16)
 
-    def soften(s, bias):
+    def column_max(s):
+        m, n = s.shape
+        return jnp.max(s.reshape(m // 8, 8, n), axis=0)
+
+    def soften(s, bias, last=None, last_bias=None):
         n = s.shape[1]
-        parts = [s[p * blk : (p + 1) * blk] for p in range(GROUP)]
-        last = jnp.where(tail, s[total:], NEG)
-        tops = [jnp.max(p.reshape(blk // 8, 8, n), axis=0) + b for p, b in zip(parts, bias)]
-        tops.append(jnp.max(last.reshape(EXTRA // 8, 8, n), axis=0))
-        top = tops[0]
-        for t in tops[1:]:
-            top = jnp.maximum(top, t)
+        parts = [s[p * blk : (p + 1) * blk] for p in range(GROUP - 1)]
+        extra = jnp.where(tail, s[total:late], NEG)
+        top = column_max(extra)
+        for q, b in zip(parts, bias):
+            top = jnp.maximum(top, column_max(q) + b)
+        if last is not None:
+            top = jnp.maximum(top, column_max(last) + last_bias)
         top = jnp.max(top, axis=0, keepdims=True)
         p = [jnp.exp2(q + (b - top)).astype(BF16) for q, b in zip(parts, bias)]
-        p.append(jnp.exp2(last - top).astype(BF16))
-        p.append(jnp.zeros((keys - rows, n), BF16))
-        return jnp.concatenate(p, axis=0)
+        p.append(jnp.exp2(extra - top).astype(BF16))
+        p.append(jnp.zeros((128 - EXTRA, n), BF16))
+        if last is not None:
+            p.append(jnp.exp2(last + (last_bias - top)).astype(BF16))
+        return jnp.concatenate(p, axis=0), top
+
+    def merge(last, bias, o, top, v):
+        best = jnp.maximum(top, jnp.max(column_max(last), axis=0, keepdims=True) + bias)
+        p = jnp.exp2(last + (bias - best)).astype(BF16)
+        scale = jnp.exp2(top - best)
+        return o * scale + dot(v, p)
 
     def scores(a, b):
         return lax.dot_general(a, b, (((1,), (1,)), ((), ())), preferred_element_type=F32)
 
-    def score(item):
-        r, j = item
-        if r is None:
-            return scores(k[...], qb[...])
+    def queries(r, j):
         at = pl.ds(place[r], blk)
         cols = slice(j * 128, (j + 1) * 128)
-        both = jnp.concatenate([qm[0, at, cols], qm[1, at, cols]], axis=0)
-        return scores(k[:, cols], both)
-
-    def mix(item, s):
-        r, j = item
-        if r is None:
-            mix_small(s)
-            return
-        at = pl.ds(place[r], blk)
-        cols = slice(j * 128, (j + 1) * 128)
-        p = soften(s, [seen(mode[r], b) for b in order])
-        o = dot(vt[j], p)
+        return jnp.concatenate([qm[0, at, cols], qm[1, at, cols]], axis=0)
+
+    early = pl.ds(0, late)
+    split = total + 128
+    step = lax.rem(lax.broadcasted_iota(jnp.int32, (1, 2 * pairs * EXTRA), 1), EXTRA)
+    audio = (step >= nb) & (step < 2 * nb)
+
+    def seen_small(b):
+        return jnp.where(audio, seen(1, b), seen(0, b))
+
+    def store(r, j, o):
         under = 1.0 / o[128:129]
         d = HEAD_DIM
         o = jnp.concatenate([o[:d, :blk] * under[:, :blk], o[d : 2 * d, blk:] * under[:, blk:]], axis=0)
-        ctx[at, cols] = o.T.astype(BF16)
-
-    def mix_small(s):
-        n = 2 * pairs * EXTRA
-        step = lax.rem(lax.broadcasted_iota(jnp.int32, (1, n), 1), EXTRA)
-        audio = (step >= nb) & (step < 2 * nb)
-        p = soften(s, [jnp.where(audio, seen(1, b), seen(0, b)) for b in order])
-        for j in range(pairs):
-            o = dot(vt[j], p)
-            o = (o[:128] * (1.0 / o[128:129])).T
-            at = 2 * j * EXTRA
-            e = jnp.where(low[:, :128], o[at : at + EXTRA], o[at + EXTRA : at + 2 * EXTRA])
-            e = 0.5 * (e + pltpu.roll(e, EXTRA - nb, 0))
-            ctx[pl.ds(total, EXTRA), j * 128 : (j + 1) * 128] = e.astype(BF16)
+        ctx[pl.ds(place[r], blk), j * 128 : (j + 1) * 128] = o.T.astype(BF16)
+
+    def first_score(item):
+        r, j = item
+        return scores(k[early, j * 128 : (j + 1) * 128], queries(r, j))
+
+    def first_mix(item, s):
+        r, j = item
+        p, top = soften(s, [seen(mode[r], b) for b in order])
+        part_top[r - 1, j] = top
+        part[r - 1, j] = dot(vt[j, :, :split], p)
+
+    def last_score(item):
+        r, j = item
+        if r is None:
+            return scores(k[early], qb[...]), scores(k[span[3]], qb[...])
+        cols = slice(j * 128, (j + 1) * 128)
+        q = queries(r, j)
+        last = scores(k[span[3], cols], q)
+        return (scores(k[early, cols], q), last) if r in (0, 3) else last
+
+    def last_mix(item, s):
+        r, j = item
+        if r is None:
+            p, _ = soften(s[0], [seen_small(b) for b in order], s[1], seen_small(3))
+            o = [dot(vt[i], p) for i in range(pairs)]
+            for i in range(pairs):
+                t = (o[i][:128] * (1.0 / o[i][128:129])).T
+                at = 2 * i * EXTRA
+                e = jnp.where(low[:, :128], t[at : at + EXTRA], t[at + EXTRA : at + 2 * EXTRA])
+                e = 0.5 * (e + pltpu.roll(e, EXTRA - nb, 0))
+                ctx[pl.ds(total, EXTRA), i * 128 : (i + 1) * 128] = e.astype(BF16)
+        elif r in (0, 3):
+            p, _ = soften(s[0], [seen(mode[r], b) for b in order], s[1], seen(mode[r], 3))
+            store(r, j, dot(vt[j], p))
+        else:
+            store(r, j, merge(s, seen(mode[r], 3), part[r - 1, j], part_top[r - 1, j], vt[j, :, split:]))
+
+    def stream(items, score, mix, look, ahead=()):
+        waiting = dict(enumerate(ahead))
+        for t in range(len(items) + look):
+            if len(ahead) <= t < len(items):
+                waiting[t] = score(items[t])
+            if t >= look:
+                mix(items[t - look], waiting.pop(t - look))
 
     def project_out(r):
         c = ctx[span[r]]
@@ -284,7 +331,6 @@
             y = dot(c, wout[h])
             ps1[h, span[r]] = y.astype(BF16)
             own1[h, span[r]] = y
-        proj[r].start()
 
     def normed_after(r):
         at = span[r]
@@ -300,11 +346,11 @@
         for t in range(tiles):
             act[span[r], t * width : (t + 1) * width] = gelu(dot(n, wup[t])).astype(BF16)
 
-    def shrink(r):
-        a = act[span[r]]
-        ps2[span[r]] = dot(a, wdown[peer]).astype(BF16)
-        down[r].start()
-        own2[span[r]] = dot(a, wdown[core])
+    def shrink_peer(r):
+        ps2[span[r]] = dot(act[span[r]], wdown[peer]).astype(BF16)
+
+    def shrink_own(r):
+        own2[span[r]] = dot(act[span[r]], wdown[core])
 
     def finish(r):
         at = span[r]
@@ -320,67 +366,100 @@
         load_qkv.wait()
         share[0].wait_recv()
     with SCOPE("project0"):
-        project(0)
+        project(0, norm(0))
     for r in (1, 2):
         with SCOPE("arr%d" % r):
             arrive[r].wait_recv()
         share[r].start()
+
+    def pass_on():
+        arrive[3].wait_recv()
+        share[3].start()
+
+    pl.when(core == 1)(pass_on)
     for r in (1, 2):
         with SCOPE("sh%d" % r):
             share[r].wait_recv()
-        with SCOPE("project%d" % r):
-            project(r)
+    soon = [(r, j) for r in (1, 2) for j in range(pairs)]
+    with SCOPE("early"):
+        n1 = norm(1)
+        n2 = norm(2)
+        project(1, n1)
+        project(2, n2)
+        stream(soon, first_score, first_mix, LOOK)
     with SCOPE("arr3"):
-        arrive[3].wait_recv()
-    share[3].start()
+        pl.when(core == 0)(pass_on)
     with SCOPE("ldwait"):
         for c in (*load_out, *load_up, *load_down):
             c.wait()
     with SCOPE("sh3"):
         share[3].wait_recv()
-    items = [(r, j) for r in (3, 1, 2, 0) for j in range(pairs)]
-    items.insert(3 * pairs, (None, 0))
-    emit_out = {(1, 1): 3, (2, 1): 1, (0, 1): 2}
-    with SCOPE("attention"):
-        project(3)
-        waiting = {}
-        for t in range(len(items) + LOOK):
-            if t < len(items):
-                waiting[t] = score(items[t])
-            if t >= LOOK:
-                mix(items[t - LOOK], waiting.pop(t - LOOK))
-                if items[t - LOOK] in emit_out:
-                    project_out(emit_out[items[t - LOOK]])
-        project_out(0)
-    with SCOPE("wproj31"):
+    with SCOPE("late3"):
+        mine = [(3, j) for j in range(pairs)]
+        ahead = []
+        project(3, norm(3), lambda: ahead.extend(last_score(i) for i in mine[:LOOK]))
+        stream(mine, last_score, last_mix, LOOK, ahead)
+        project_out(3)
+    proj[3].start()
+    with SCOPE("late12"):
+        stream(soon + [(None, 0)], last_score, last_mix, LOOK + 2)
+        project_out(1)
+    proj[1].start()
+    with SCOPE("wproj3"):
         proj[3].wait_recv()
+    with SCOPE("ffn3"):
+        n = normed_after(3)
+        project_out(2)
+        grow(3, n)
+        shrink_peer(3)
+    proj[2].start()
+    down[3].start()
+    with SCOPE("wproj1"):
         proj[1].wait_recv()
-    with SCOPE("ffnA"):
-        grow(3, normed_after(3))
-        n = normed_after(1)
-        shrink(3)
-        grow(1, n)
+    with SCOPE("ffn1"):
+        shrink_own(3)
+        grow(1, normed_after(1))
+        shrink_peer(1)
+    down[1].start()
     with SCOPE("wB"):
+        down[3].wait_recv()
+    with SCOPE("fin3"):
+        finish(3)
+    with SCOPE("wC"):
         proj[2].wait_recv()
-        down[3].wait_recv()
-    with SCOPE("ffnB"):
-        finish(3)
-        n = normed_after(2)
-        shrink(1)
-        grow(2, n)
-    with SCOPE("wC"):
-        proj[0].wait_recv()
+    with SCOPE("ffn2"):
+        shrink_own(1)
+        grow(2, normed_after(2))
+        shrink_peer(2)
+    down[2].start()
+    with SCOPE("wC1"):
         down[1].wait_recv()
-    with SCOPE("ffnC"):
+    with SCOPE("fin1"):
         finish(1)
-        n = normed_after(0)
-        shrink(2)
-        grow(0, n)
+    with SCOPE("att0"):
+        shrink_own(2)
+        ours = [(0, j) for j in range(pairs)]
+        ahead = [last_score(i) for i in ours[:3]]
+        for i in range(2):
+            last_mix(ours[i], ahead[i])
     with SCOPE("wD"):
         down[2].wait_recv()
-    with SCOPE("ffnD"):
+    with SCOPE("fin2"):
         finish(2)
-        shrink(0)
+    with SCOPE("atts"):
+        stream(ours[2:], last_score, last_mix, LOOK, ahead[2:])
+        project_out(0)
+    proj[0].start()
+    with SCOPE("wC0"):
+        proj[0].wait_recv()
+    with SCOPE("ffn0"):
+        n = normed_after(0)
+        grow(0, n)
+    with SCOPE("down0"):
+        shrink_peer(0)
+    down[0].start()
+    with SCOPE("own0"):
+        shrink_own(0)
     with SCOPE("wE"):
         down[0].wait_recv()
     with SCOPE("fin0"):
@@ -458,6 +537,8 @@
             V((2 * pairs * EXTRA, inner), BF16),
             V((rows, inner), BF16),
             V((pairs, 128 + EXTRA, keys), BF16),
+            V((2, pairs, 128 + EXTRA, 2 * blk), F32),
+            V((2, pairs, 1, 2 * blk), F32),
             V((rows, inner), BF16),
             V((2, rows, width), BF16),
             V((2, rows, width), BF16),

time: 31 us -> 28.9 us (0.932)
  Pallas kernels: 30.2 us -> 28.1 us
    pallas_call x1, Pallas kernels: 29.5 us -> 27.3 us  [body(): pl.pallas_call(functools.partial(kernel, blk, nb), out_shape=(jax.ShapeDt...]
where the time goes in v2:
time: 28.9 us; the launch traced here: 28.7 us
  Pallas kernels  28.1 us (97%)
  between operations  0.64 us (2%)
    pallas_call x1, Pallas kernels, body(): pl.pallas_call(functools.partial(kernel, blk, nb), out_shape=(jax.ShapeDt...  27.3 us
    pallas_call x1, Pallas kernels, body(): pl.pallas_call(place, out_shape=(jax.ShapeDtypeStruct(tokens.shape, BF16)...  0.77 us

profile of v2, /device:TPU:0, one launch (start us, length us, event | category | flops | bytes accessed | tf_op | source)
XLA Modules:
  0.0 28.7 jit_solution(17915659872074959209)
XLA Ops:
  0.6 27.3 %merge_layer.1 = (bf16[3,128,512]{2,1,0:T(8,128)(2,1)S(1)}, bf16[1,4,512]{2,1,0:T(4,128)(2,1)S(1)}) custom-call(s32[16]{0:T(128)} %video_hbm.1, s32[3,16]{1,0:T(4,128)} %bitcast.5, bf16[3,128,512]{2,1,0:T(8,128)(2,1)} %tok_hbm.1, bf16[1,4,512]{2,1,0:T(4,128)(2,1)} %bot_hbm.1, f32[1,1024]{1,0:T(1,128)} %bitcast.3, f32[1,1024]{1,0:T(1,128)} %bitcast.4, ...), custom_call_target="tpu_custom_call" | custom-call | tf_op jit(solution)/shard_map/merge_layer/pallas_call | solution.py:514
  28.0 0.8 %place.1 = (bf16[3,128,512]{2,1,0:T(8,128)(2,1)}, bf16[1,4,512]{2,1,0:T(4,128)(2,1)}) custom-call(bf16[3,128,512]{2,1,0:T(8,128)(2,1)S(1)} %get-tuple-element.4.stored_ref, bf16[1,4,512]{2,1,0:T(4,128)(2,1)S(1)} %get-tuple-element.5.merged_ref), custom_call_target="tpu_custom_call" | custom-call | tf_op jit(solution)/shard_map/place/pallas_call | solution.py:576

commit v3 on v2

--- a/solution.py
+++ b/solution.py
@@ -120,11 +120,11 @@
         load(4, g1_hbm, g1_ref),
         load(5, g2_hbm, g2_ref),
     ]
-    load_qkv = load(6, wqkv_hbm, wqkv)
+    load_qkv = load(0, wqkv_hbm, wqkv)
     tiles = wup.shape[0]
-    load_out = [load(7 + h, wout_hbm.at[:, halves[h]], wout.at[h]) for h in range(2)]
-    load_down = [load(9 + h, wdown_hbm.at[:, halves[h]], wdown.at[h]) for h in range(2)]
-    load_up = [load(11 + t, wup_hbm.at[:, pl.ds(t * width, width)], wup.at[t]) for t in range(tiles)]
+    load_out = [load(1 + h, wout_hbm.at[:, halves[h]], wout.at[h]) for h in range(2)]
+    load_down = [load(3 + h, wdown_hbm.at[:, halves[h]], wdown.at[h]) for h in range(2)]
+    load_up = [load(5 + t, wup_hbm.at[:, pl.ds(t * width, width)], wup.at[t]) for t in range(tiles)]
     for c in first:
         c.start()
 
@@ -163,30 +163,30 @@
     lanes = [2 * blk, 0, blk, total + 128]
     span = [pl.ds(place[0], blk + EXTRA)] + [pl.ds(place[r], blk) for r in range(1, GROUP)]
 
-    def ici(r, src, dst, base):
+    def ici(r, src, dst, sent, got):
         return pltpu.make_async_remote_copy(
             src_ref=src,
             dst_ref=dst,
-            send_sem=send_sem.at[base + r],
-            recv_sem=recv_sem.at[base + r],
+            send_sem=send_sem.at[sent + r],
+            recv_sem=recv_sem.at[got + r],
             device_id={"clip": partner[r]},
         )
 
-    def d2d(r, src, dst, base):
+    def d2d(r, src, dst, sent, got):
         return pltpu.make_async_remote_copy(
             src_ref=src,
             dst_ref=dst,
-            send_sem=send_sem.at[base + r],
-            recv_sem=recv_sem.at[base + r],
+            send_sem=send_sem.at[sent + r],
+            recv_sem=recv_sem.at[got + r],
             device_id={"mp": peer},
         )
 
     half = x.at[core]
-    arrive = [ici(r, snd.at[r - 1], half.at[span[r]], 0) if r else None for r in range(GROUP)]
-    share = [d2d(r, half.at[span[r]], half.at[span[r]], 4) for r in range(GROUP)]
-    proj = [d2d(r, ps1.at[:, span[r]], pr1.at[:, span[r]], 8) for r in range(GROUP)]
-    down = [d2d(r, ps2.at[span[r]], pr2.at[span[r]], 12) for r in range(GROUP)]
-    back = [ici(r, fin.at[r - 1], ret.at[r], 16) if r else None for r in range(GROUP)]
+    arrive = [ici(r, snd.at[r - 1], half.at[span[r]], -1, -1) if r else None for r in range(GROUP)]
+    share = [d2d(r, half.at[span[r]], half.at[span[r]], 3, 3) for r in range(GROUP)]
+    proj = [d2d(r, ps1.at[:, span[r]], pr1.at[:, span[r]], 7, 7) for r in range(GROUP)]
+    down = [d2d(r, ps2.at[span[r]], pr2.at[span[r]], 3, 11) for r in range(GROUP)]
+    back = [ici(r, fin.at[r - 1], ret.at[r], -1, 14) if r else None for r in range(GROUP)]
 
     for r in range(1, GROUP):
         snd[r - 1] = tok[pick[r]]
@@ -238,8 +238,9 @@
 
     def soften(s, bias, last=None, last_bias=None):
         n = s.shape[1]
-        parts = [s[p * blk : (p + 1) * blk] for p in range(GROUP - 1)]
-        extra = jnp.where(tail, s[total:late], NEG)
+        m = len(bias)
+        parts = [s[p * blk : (p + 1) * blk] for p in range(m)]
+        extra = jnp.where(tail, s[m * blk : m * blk + EXTRA], NEG)
         top = column_max(extra)
         for q, b in zip(parts, bias):
             top = jnp.maximum(top, column_max(q) + b)
@@ -253,11 +254,15 @@
             p.append(jnp.exp2(last + (last_bias - top)).astype(BF16))
         return jnp.concatenate(p, axis=0), top
 
-    def merge(last, bias, o, top, v):
-        best = jnp.maximum(top, jnp.max(column_max(last), axis=0, keepdims=True) + bias)
-        p = jnp.exp2(last + (bias - best)).astype(BF16)
-        scale = jnp.exp2(top - best)
-        return o * scale + dot(v, p)
+    def merge(lasts, bias, o, top, v):
+        best = top
+        for q, b in zip(lasts, bias):
+            best = jnp.maximum(best, jnp.max(column_max(q), axis=0, keepdims=True) + b)
+        o = o * jnp.exp2(top - best)
+        p = [jnp.exp2(q + (b - best)).astype(BF16) for q, b in zip(lasts, bias)]
+        if len(p) > 1:
+            o = o + dot(v[:, : 2 * blk], jnp.concatenate(p[:2], axis=0))
+        return o + dot(v[:, split:], p[-1])
 
     def scores(a, b):
         return lax.dot_general(a, b, (((1,), (1,)), ((), ())), preferred_element_type=F32)
@@ -269,6 +274,7 @@
 
     early = pl.ds(0, late)
     split = total + 128
+    own_keys = pl.ds(place[0], blk + EXTRA)
     step = lax.rem(lax.broadcasted_iota(jnp.int32, (1, 2 * pairs * EXTRA), 1), EXTRA)
     audio = (step >= nb) & (step < 2 * nb)
 
@@ -283,13 +289,19 @@
 
     def first_score(item):
         r, j = item
-        return scores(k[early, j * 128 : (j + 1) * 128], queries(r, j))
+        seen_keys = own_keys if r == 0 else early
+        return scores(k[seen_keys, j * 128 : (j + 1) * 128], queries(r, j))
 
     def first_mix(item, s):
         r, j = item
-        p, top = soften(s, [seen(mode[r], b) for b in order])
-        part_top[r - 1, j] = top
-        part[r - 1, j] = dot(vt[j, :, :split], p)
+        if r == 0:
+            p, top = soften(s, [seen(mode[0], 0)])
+            v = vt[j, :, 2 * blk : split]
+        else:
+            p, top = soften(s, [seen(mode[r], b) for b in order])
+            v = vt[j, :, :split]
+        part_top[r, j] = top
+        part[r, j] = dot(v, p)
 
     def last_score(item):
         r, j = item
@@ -298,7 +310,12 @@
         cols = slice(j * 128, (j + 1) * 128)
         q = queries(r, j)
         last = scores(k[span[3], cols], q)
-        return (scores(k[early, cols], q), last) if r in (0, 3) else last
+        if r == 3:
+            return scores(k[early, cols], q), last
+        if r == 0:
+            s = scores(k[: 2 * blk, cols], q)
+            return s[:blk], s[blk:], last
+        return (last,)
 
     def last_mix(item, s):
         r, j = item
@@ -311,11 +328,12 @@
                 e = jnp.where(low[:, :128], t[at : at + EXTRA], t[at + EXTRA : at + 2 * EXTRA])
                 e = 0.5 * (e + pltpu.roll(e, EXTRA - nb, 0))
                 ctx[pl.ds(total, EXTRA), i * 128 : (i + 1) * 128] = e.astype(BF16)
-        elif r in (0, 3):
-            p, _ = soften(s[0], [seen(mode[r], b) for b in order], s[1], seen(mode[r], 3))
+        elif r == 3:
+            p, _ = soften(s[0], [seen(mode[3], b) for b in order], s[1], seen(mode[3], 3))
             store(r, j, dot(vt[j], p))
         else:
-            store(r, j, merge(s, seen(mode[r], 3), part[r - 1, j], part_top[r - 1, j], vt[j, :, split:]))
+            bias = [seen(mode[r], b) for b in ((1, 2, 3) if r == 0 else (3,))]
+            store(r, j, merge(s, bias, part[r, j], part_top[r, j], vt[j]))
 
     def stream(items, score, mix, look, ahead=()):
         waiting = dict(enumerate(ahead))
@@ -367,6 +385,7 @@
         share[0].wait_recv()
     with SCOPE("project0"):
         project(0, norm(0))
+        stream([(0, j) for j in range(pairs)], first_score, first_mix, LOOK)
     for r in (1, 2):
         with SCOPE("arr%d" % r):
             arrive[r].wait_recv()
@@ -406,6 +425,10 @@
         project_out(1)
     proj[1].start()
     with SCOPE("wproj3"):
+        for r in range(GROUP):
+            share[r].wait_send()
+            if r:
+                arrive[r].wait_send()
         proj[3].wait_recv()
     with SCOPE("ffn3"):
         n = normed_after(3)
@@ -455,7 +478,6 @@
     with SCOPE("ffn0"):
         n = normed_after(0)
         grow(0, n)
-    with SCOPE("down0"):
         shrink_peer(0)
     down[0].start()
     with SCOPE("own0"):
@@ -464,27 +486,33 @@
         down[0].wait_recv()
     with SCOPE("fin0"):
         finish(0)
+    for r in range(1, GROUP):
+        back[r].wait_send()
+    for r in range(GROUP):
+        for c in (proj, down):
+            c[r].wait_send()
     with SCOPE("backwait"):
         for r in (3, 1, 2):
             back[r].wait_recv()
-    for s in range(slots):
-        where = jnp.int32(0)
-        for r in range(GROUP):
-            where = jnp.where(own[s] == partner[r], r, where)
-        live = jnp.where(entry[s] >= 0, 1.0, 0.0).astype(F32)
-        block = ret[where].astype(F32)
-        out_ref[s] = (block * live).astype(BF16)
-    for r in range(1, GROUP):
-        arrive[r].wait_send()
-        back[r].wait_send()
-    for r in range(GROUP):
-        for c in (share, proj, down):
-            c[r].wait_send()
-
-
-def place(stored_ref, merged_ref, out_ref, outb_ref):
-    out_ref[...] = stored_ref[...]
-    outb_ref[...] = merged_ref[...]
+    with SCOPE("select"):
+        for s in range(slots):
+            where = jnp.int32(0)
+            for r in range(GROUP):
+                where = jnp.where(own[s] == partner[r], r, where)
+            live = jnp.where(entry[s] >= 0, 1.0, 0.0).astype(F32)
+            block = ret[where].astype(F32)
+            out_ref[s] = (block * live).astype(BF16)
+
+
+def place(stored_ref, merged_ref, out_hbm, outb_hbm, sem):
+    copies = [
+        pltpu.make_async_copy(stored_ref, out_hbm, sem.at[0]),
+        pltpu.make_async_copy(merged_ref, outb_hbm, sem.at[1]),
+    ]
+    for c in copies:
+        c.start()
+    for c in copies:
+        c.wait()
 
 
 def body(
@@ -537,8 +565,8 @@
             V((2 * pairs * EXTRA, inner), BF16),
             V((rows, inner), BF16),
             V((pairs, 128 + EXTRA, keys), BF16),
-            V((2, pairs, 128 + EXTRA, 2 * blk), F32),
-            V((2, pairs, 1, 2 * blk), F32),
+            V((GROUP - 1, pairs, 128 + EXTRA, 2 * blk), F32),
+            V((GROUP - 1, pairs, 1, 2 * blk), F32),
             V((rows, inner), BF16),
             V((2, rows, width), BF16),
             V((2, rows, width), BF16),
@@ -550,9 +578,9 @@
             V((rows, width), F32),
             V((GROUP - 1, blk, width), BF16),
             V((GROUP, blk, width), BF16),
-            pltpu.SemaphoreType.DMA((11 + ff // width,)),
-            pltpu.SemaphoreType.DMA((20,)),
-            pltpu.SemaphoreType.DMA((20,)),
+            pltpu.SemaphoreType.DMA((max(6, 5 + ff // width),)),
+            pltpu.SemaphoreType.DMA((11,)),
+            pltpu.SemaphoreType.DMA((18,)),
         ],
         compiler_params=pltpu.CompilerParams(collective_id=0, has_side_effects=True, vmem_limit_bytes=40 << 20),
         name="merge_layer",
@@ -580,7 +608,8 @@
             jax.ShapeDtypeStruct(bottleneck.shape, BF16),
         ),
         in_specs=[vmem, vmem],
-        out_specs=(vmem, vmem),
+        out_specs=(hbm, hbm),
+        scratch_shapes=[pltpu.SemaphoreType.DMA((2,))],
         compiler_params=pltpu.CompilerParams(vmem_limit_bytes=4 << 20),
         name="place",
     )(stored, merged)

time: 28.9 us -> 28.7 us (level)
  no operation moved by 1% of the time
where the time goes in v3:
time: 28.7 us; the launch traced here: 28.6 us
  Pallas kernels  27.9 us (97%)
  between operations  0.64 us (2%)
    pallas_call x1, Pallas kernels, body(): pl.pallas_call(functools.partial(kernel, blk, nb), out_shape=(jax.ShapeDt...  27.1 us
    pallas_call x1, Pallas kernels, body(): pl.pallas_call(place, out_shape=(jax.ShapeDtypeStruct(tokens.shape, BF16)...  0.77 us

profile of v3, /device:TPU:0, one launch (start us, length us, event | category | flops | bytes accessed | tf_op | source)
XLA Modules:
  0.0 28.6 jit_solution(11851860908352527912)
XLA Ops:
  0.6 27.1 %merge_layer.1 = (bf16[3,128,512]{2,1,0:T(8,128)(2,1)S(1)}, bf16[1,4,512]{2,1,0:T(4,128)(2,1)S(1)}) custom-call(s32[16]{0:T(128)} %video_hbm.1, s32[3,16]{1,0:T(4,128)} %bitcast.5, bf16[3,128,512]{2,1,0:T(8,128)(2,1)} %tok_hbm.1, bf16[1,4,512]{2,1,0:T(4,128)(2,1)} %bot_hbm.1, f32[1,1024]{1,0:T(1,128)} %bitcast.3, f32[1,1024]{1,0:T(1,128)} %bitcast.4, ...), custom_call_target="tpu_custom_call" | custom-call | tf_op jit(solution)/shard_map/merge_layer/pallas_call | solution.py:542
  27.8 0.8 %place.1 = (bf16[3,128,512]{2,1,0:T(8,128)(2,1)}, bf16[1,4,512]{2,1,0:T(4,128)(2,1)}) custom-call(bf16[3,128,512]{2,1,0:T(8,128)(2,1)S(1)} %get-tuple-element.4.stored_ref, bf16[1,4,512]{2,1,0:T(4,128)(2,1)S(1)} %get-tuple-element.5.merged_ref), custom_call_target="tpu_custom_call" | custom-call | tf_op jit(solution)/shard_map/place/pallas_call | solution.py:604
